TPU v7x, 32 devices: a whole 2x2x4 slice. The times are simulated.
32 devices in a mesh: pb: 2 (over x), ka: 16 (over z, y, core).
Axes of the slice: x: 2, y: 2, z: 4, core: 2. Of those that a mesh axis runs over, the one named last changes fastest.
Arguments:
- coupling: bfloat16 [2, 16, 32, 32, 384], P('pb', 'ka'), may hold values from -0.796875 to 0.796875
- phonon_occ: float32 [2, 16, 32, 12], P('pb', 'ka'), may hold values from 0.1 to 1
- band_window: int32 [2, 16, 32, 32], P('pb', 'ka'), may hold values 0 or 1
- pair_count: int32 [2, 16, 16], P('pb', 'ka'), may hold values from 0 to 2, as said below
- k_target: int32 [2, 16, 32], P('pb', 'ka'), may hold values from 0 to 127
- kq_source: int32 [2, 16, 32], P('pb', 'ka'), may hold values from 0 to 127
- velocity: float32 [3, 32, 2048], P(None, None, 'ka'), may hold values from -6 to 6
- lifetime: float32 [32, 2048], P(None, 'ka'), may hold values from 0.5 to 2
Outputs:
- deviation: float32 [3, 32, 2048], P(None, None, 'ka')
Inputs may be any that keep to these rules, and one draw needn't show every extreme that they name: pair_count[p, a, d] is the number of live tile slots among slots d * 2 to d * 2 + 1 of device (p, a); in every q-group p some owner d receives 2 live tiles from every source.
All inputs are finite; a program needn't handle non-finite values. No bound on the sum of `band_window` on one device may be relied on, other than what follows from the above.
Results may differ from a plain program's by a relative error of at most 0.012.
Values may be sent and summed in bfloat16 or wider, within the bound.
A program may use at most 64 MiB of HBM per device.

v0:
```python
import jax
import jax.numpy as jnp
from jax import lax
from jax.sharding import PartitionSpec as P

MODES = 12
TILE_SLOTS = 2
ITERS = 4


def tile_terms(weight, chosen):
    return jnp.einsum("tnm,dmt->dnt", weight, chosen, preferred_element_type=jnp.float32)


def shards(coupling, phonon_occ, band_window, pair_count, k_target, kq_source, velocity, lifetime):
    tile_count = coupling.shape[2]
    block_width = velocity.shape[2]
    directions = velocity.shape[0]
    band_count = velocity.shape[1]
    slot_live = (
        (jnp.arange(TILE_SLOTS)[None, :] < pair_count[0, 0][:, None])
        .reshape(tile_count)
        .astype(jnp.float32)
    )
    window = band_window[0, 0].astype(jnp.float32) * slot_live[:, None]
    widened = coupling[0, 0].astype(jnp.float32)
    squared = (widened * widened).reshape(tile_count, band_count, band_count, MODES)
    summed = jnp.sum(squared * phonon_occ[0, 0][:, None, None, :], axis=3)
    weight = (summed * window[:, :, None]).astype(jnp.bfloat16)
    targets = lax.all_to_all(k_target[0, 0], "ka", split_axis=0, concat_axis=0, tiled=True)
    onehot = (targets[:, None] == jnp.arange(block_width, dtype=jnp.int32)[None, :]).astype(
        jnp.float32
    )
    deviation = lifetime[None] * velocity
    for iteration in range(ITERS):
        rounded = deviation.astype(jnp.bfloat16)
        local_terms = tile_terms(weight, jnp.take(rounded, kq_source[0, 0], axis=2))
        contribution = lax.all_to_all(
            local_terms.astype(jnp.bfloat16), "ka", split_axis=2, concat_axis=2, tiled=True
        ).astype(local_terms.dtype)
        partial_value = jnp.dot(
            contribution.reshape(directions * band_count, tile_count),
            onehot,
            precision=lax.Precision.HIGHEST,
            preferred_element_type=jnp.float32,
        )
        partial_value = partial_value.reshape(directions, band_count, block_width)
        scattering = lax.psum(partial_value.astype(jnp.bfloat16), "pb").astype(jnp.float32)
        deviation = lifetime[None] * (velocity + scattering)
    return deviation


def solution(mesh):
    placed = (
        P("pb", "ka", None, None, None),
        P("pb", "ka", None, None),
        P("pb", "ka", None, None),
        P("pb", "ka", None),
        P("pb", "ka", None),
        P("pb", "ka", None),
        P(None, None, "ka"),
        P(None, "ka"),
    )
    return jax.shard_map(
        shards, mesh=mesh, in_specs=placed, out_specs=P(None, None, "ka"), check_vma=False
    )
```

profile of v0, /device:TPU:0, one launch (start us, length us, event | category | flops | bytes accessed | tf_op | source)
XLA Modules:
  0.0 100.8 jit_solution(7904888660373477923)
XLA Ops:
  0.5 1.3 %reduce.6 = s32[32]{0:T(128)S(1)} reduce(s32[1,1,32]{2,1,0:T(1,128)} %param.14, s32[]{:T(128)} %broadcast.93), dimensions={0,1}, to_apply=%param.14.reduce_sub_computation.3 | reduce | bytes 260 | tf_op args[4]
  1.9 0.7 all_to_all.19
  2.5 7.4 %all-to-all-start.1 = ((s32[16,2,1]{1,2,0:T(1,128)}), s32[16,2,1]{1,2,0:T(1,128)S(1)}, u32[]{:S(2)}, u32[]{:S(2)}) async-start(s32[16,2,1]{1,2,0:T(1,128)} %bitcast.6), calls=%async_computation.1 | async-start | bytes 16384 | tf_op jit(solution)/shard_map/all_to_all | solution.py:30
  10.0 0.7 compare_select_fusion
  10.6 0.7 compare_and_fusion
  11.3 1.3 %convert_multiply_fusion = f32[1,1,32,32,384]{4,3,2,1,0:T(8,128)S(1)} fusion(bf16[1,1,32,32,384]{4,3,2,1,0:T(8,128)(2,1)} %param.10), kind=kLoop, calls=%fused_computation.5 | loop fusion | flops 786432 | bytes 2359296 | tf_op jit(solution)/shard_map/mul | solution.py:27
  12.6 5.9 %copy.30 = f32[1,1,32,32,384]{3,2,4,1,0:T(8,128)} copy(f32[1,1,32,32,384]{4,3,2,1,0:T(8,128)S(1)} %convert_multiply_fusion) | data formatting | bytes 3145728 | tf_op jit(solution)/shard_map/mul | solution.py:27
  18.8 3.7 %multiply_reduce_fusion = f32[32,32,32]{1,0,2:T(8,128)S(1)} fusion(f32[32,32,32,12]{1,0,3,2:T(8,128)} %bitcast.43, f32[32,12]{0,1:T(8,128)S(1)} %bitcast.44), kind=kLoop, calls=%fused_computation.4 | loop fusion | flops 753664 | bytes 1705472 | tf_op jit(solution)/shard_map/reduce_sum | solution.py:28
  23.1 0.6 gather_fusion
  23.7 0.9 fusion
  24.7 6.0 %all-to-all-start = ((bf16[3,32,32]{1,0,2:T(4,128)(2,1)}), bf16[3,32,32]{1,0,2:T(4,128)(2,1)S(1)}, u32[]{:S(2)}, u32[]{:S(2)}) async-start(bf16[3,32,32]{1,0,2:T(4,128)(2,1)} %fusion), calls=%async_computation | async-start | bytes 65536 | tf_op jit(solution)/shard_map/all_to_all | solution.py:38
  30.7 0.7 reduce.7
  31.5 5.9 %all-to-all-done = bf16[3,32,32]{1,0,2:T(4,128)(2,1)S(1)} async-done(((bf16[3,32,32]{1,0,2:T(4,128)(2,1)}), bf16[3,32,32]{1,0,2:T(4,128)(2,1)S(1)}, u32[]{:S(2)}, u32[]{:S(2)}) %all-to-all-start) | async-done | bytes 6176 | tf_op jit(solution)/shard_map/all_to_all | solution.py:38
  37.5 8.4 %psum.28 = bf16[3,32,128]{2,1,0:T(8,128)(2,1)S(1)} all-reduce(bf16[3,32,128]{2,1,0:T(8,128)(2,1)S(1)} %convolution_convert_fusion.7), channel_id=1, replica_groups=mesh['pb'=2,'ka'=16] {'pb'}, use_global_device_ids=true, to_apply=%region_1.0 | all-reduce | flops 12288 | bytes 49152 | tf_op jit(solution)/shard_map/psum | solution.py:48
  46.0 0.6 gather_fusion.1
  47.0 9.2 %all_to_all.29 = bf16[3,32,32]{1,0,2:T(4,128)(2,1)S(1)} all-to-all(bf16[3,32,32]{1,0,2:T(4,128)(2,1)S(1)} %fusion.1), channel_id=1, replica_groups=mesh['pb'=2,'ka'=16] {'ka'}, dimensions={2} | all-to-all | bytes 12288 | tf_op jit(solution)/shard_map/all_to_all | solution.py:38
  56.3 7.3 %psum.29 = bf16[3,32,128]{2,1,0:T(8,128)(2,1)S(1)} all-reduce(bf16[3,32,128]{2,1,0:T(8,128)(2,1)S(1)} %convolution_convert_fusion.6), channel_id=1, replica_groups=mesh['pb'=2,'ka'=16] {'pb'}, use_global_device_ids=true, to_apply=%region_2.4 | all-reduce | flops 12288 | bytes 49152 | tf_op jit(solution)/shard_map/psum | solution.py:48
  63.8 0.6 gather_fusion.2
  64.7 9.2 %all_to_all.30 = bf16[3,32,32]{1,0,2:T(4,128)(2,1)S(1)} all-to-all(bf16[3,32,32]{1,0,2:T(4,128)(2,1)S(1)} %fusion.2), channel_id=1, replica_groups=mesh['pb'=2,'ka'=16] {'ka'}, dimensions={2} | all-to-all | bytes 12288 | tf_op jit(solution)/shard_map/all_to_all | solution.py:38
  74.1 8.5 %psum.30 = bf16[3,32,128]{2,1,0:T(8,128)(2,1)S(1)} all-reduce(bf16[3,32,128]{2,1,0:T(8,128)(2,1)S(1)} %convolution_convert_fusion.5), channel_id=1, replica_groups=mesh['pb'=2,'ka'=16] {'pb'}, use_global_device_ids=true, to_apply=%region_3.5 | all-reduce | flops 12288 | bytes 49152 | tf_op jit(solution)/shard_map/psum | solution.py:48
  82.7 0.6 gather_fusion.3
  83.6 9.2 %all_to_all.31 = bf16[3,32,32]{1,0,2:T(4,128)(2,1)S(1)} all-to-all(bf16[3,32,32]{1,0,2:T(4,128)(2,1)S(1)} %fusion.3), channel_id=1, replica_groups=mesh['pb'=2,'ka'=16] {'ka'}, dimensions={2} | all-to-all | bytes 12288 | tf_op jit(solution)/shard_map/all_to_all | solution.py:38
  93.0 7.1 %psum.31 = bf16[3,32,128]{2,1,0:T(8,128)(2,1)S(1)} all-reduce(bf16[3,32,128]{2,1,0:T(8,128)(2,1)S(1)} %convolution_convert_fusion.4), channel_id=1, replica_groups=mesh['pb'=2,'ka'=16] {'pb'}, use_global_device_ids=true, to_apply=%region_4.6 | all-reduce | flops 12288 | bytes 49152 | tf_op jit(solution)/shard_map/psum | solution.py:48
  100.1 0.6 add_multiply_fusion
  (35 shorter events, 3.6 us)
Async XLA Ops:
  0.0 18.6 %copy-start.3 = (f32[1,1,32,12]{2,1,3,0:T(1,128)S(1)}, f32[1,1,32,12]{2,1,3,0:T(1,128)}, u32[]{:S(2)}) copy-start(f32[1,1,32,12]{2,1,3,0:T(1,128)} %param.11) | copy-start | bytes 4612
  0.0 18.6 %copy-start.4 = (s32[1,1,16]{2,1,0:T(1,128)S(1)}, s32[1,1,16]{2,1,0:T(1,128)}, u32[]{:S(2)}) copy-start(s32[1,1,16]{2,1,0:T(1,128)} %param.13) | copy-start | bytes 196
  2.5 22.1 %all-to-all-start.1 = ((s32[16,2,1]{1,2,0:T(1,128)}), s32[16,2,1]{1,2,0:T(1,128)S(1)}, u32[]{:S(2)}, u32[]{:S(2)}) async-start(s32[16,2,1]{1,2,0:T(1,128)} %bitcast.6), calls=%async_computation.1 | async-start | bytes 16384 | tf_op jit(solution)/shard_map/all_to_all | solution.py:30
  12.6 9.9 %copy-start.2 = (s32[1,1,32,32]{3,2,1,0:T(8,128)S(1)}, s32[1,1,32,32]{3,2,1,0:T(8,128)}, u32[]{:S(2)}) copy-start(s32[1,1,32,32]{3,2,1,0:T(8,128)} %param.12) | copy-start | bytes 12292
  12.6 10.3 %copy-start = (f32[3,32,128]{2,1,0:T(8,128)S(1)}, f32[3,32,128]{2,1,0:T(8,128)}, u32[]{:S(2)}) copy-start(f32[3,32,128]{2,1,0:T(8,128)} %param.16) | copy-start | bytes 147460
  12.6 10.3 %copy-start.1 = (f32[32,128]{1,0:T(8,128)S(1)}, f32[32,128]{1,0:T(8,128)}, u32[]{:S(2)}) copy-start(f32[32,128]{1,0:T(8,128)} %param.17) | copy-start | bytes 49156
  24.7 12.6 %all-to-all-start = ((bf16[3,32,32]{1,0,2:T(4,128)(2,1)}), bf16[3,32,32]{1,0,2:T(4,128)(2,1)S(1)}, u32[]{:S(2)}, u32[]{:S(2)}) async-start(bf16[3,32,32]{1,0,2:T(4,128)(2,1)} %fusion), calls=%async_computation | async-start | bytes 65536 | tf_op jit(solution)/shard_map/all_to_all | solution.py:38
where the time goes:
time: 101 us
  blocking collectives  58.8 us (58%)
  starting transfers between devices  13.4 us (13%)
  local copies, waits for them, and re-layouts  10.7 us (11%)
  other arithmetic  9.2 us (9%)
  waiting for transfers between devices  5.88 us (6%)
  matrix products  2.6 us (3%)
    psum x4, blocking collectives, shards(): lax.psum(partial_value.astype(jnp.bfloat16), 'pb').astype(jnp.float32)  31.2 us
    all_to_all x3, blocking collectives, shards(): lax.all_to_all(local_terms.astype(jnp.bfloat16), 'ka', split_axis=2, conc...  27.6 us
    all_to_all x1, starting transfers between devices, shards(): lax.all_to_all(k_target[0, 0], 'ka', split_axis=0, concat_axis=0, tiled=T...  7.41 us
    all_to_all x1, starting transfers between devices, shards(): lax.all_to_all(local_terms.astype(jnp.bfloat16), 'ka', split_axis=2, conc...  6.01 us
    mul x1, local copies, waits for them, and re-layouts, shards(): widened * widened  5.94 us
    all_to_all x1, waiting for transfers between devices, shards(): lax.all_to_all(local_terms.astype(jnp.bfloat16), 'ka', split_axis=2, conc...  5.88 us
    reduce_sum x1, other arithmetic, shards(): summed = jnp.sum(squared * phonon_occ[0, 0][:, None, None, :], axis=3)  3.71 us
    gather x4, local copies, waits for them, and re-layouts, shards(): local_terms = tile_terms(weight, jnp.take(rounded, kq_source[0, 0], axis=2))  2.44 us
  transfers between devices with their start and end apart: 2, of which 1 were waited for; matrix products, arithmetic and copies ran while one was open for 15% of the time, Pallas kernels for 0%

commit v1 on v0

--- a/solution.py
+++ b/solution.py
@@ -45,7 +45,9 @@
             preferred_element_type=jnp.float32,
         )
         partial_value = partial_value.reshape(directions, band_count, block_width)
-        scattering = lax.psum(partial_value.astype(jnp.bfloat16), "pb").astype(jnp.float32)
+        scattering = jnp.sum(
+            lax.all_gather(partial_value.astype(jnp.bfloat16), "pb"), axis=0
+        ).astype(jnp.float32)
         deviation = lifetime[None] * (velocity + scattering)
     return deviation
 

time: 101 us -> 88.1 us (0.87)
  blocking collectives: 58.8 us -> 45.6 us
    psum x4 -> x0, blocking collectives: 31.2 us -> none  [shards(): lax.psum(partial_value.astype(jnp.bfloat16), 'pb').astype(jnp.float32)]
    all_gather x0 -> x4, blocking collectives: none -> 18 us  [shards(): lax.all_gather(partial_value.astype(jnp.bfloat16), 'pb')]
  transfers between devices with their start and end apart: 2 -> 2, of which waited for: 1 -> 1; matrix products, arithmetic and copies ran while one was open for 15% -> 18% of each run, Pallas kernels for 0% -> 0%
where the time goes in v1:
time: 88.1 us; the launch traced here: 87.6 us
  blocking collectives  45.6 us (52%)
  starting transfers between devices  13.4 us (15%)
  local copies, waits for them, and re-layouts  10.7 us (12%)
  other arithmetic  9.23 us (10%)
  waiting for transfers between devices  5.88 us (7%)
  matrix products  2.6 us (3%)
    all_to_all x3, blocking collectives, shards(): lax.all_to_all(local_terms.astype(jnp.bfloat16), 'ka', split_axis=2, conc...  27.6 us
    all_gather x4, blocking collectives, shards(): lax.all_gather(partial_value.astype(jnp.bfloat16), 'pb')  18 us
    all_to_all x1, starting transfers between devices, shards(): lax.all_to_all(k_target[0, 0], 'ka', split_axis=0, concat_axis=0, tiled=T...  7.41 us
    all_to_all x1, starting transfers between devices, shards(): lax.all_to_all(local_terms.astype(jnp.bfloat16), 'ka', split_axis=2, conc...  6.01 us
    mul x1, local copies, waits for them, and re-layouts, shards(): widened * widened  5.94 us
    all_to_all x1, waiting for transfers between devices, shards(): lax.all_to_all(local_terms.astype(jnp.bfloat16), 'ka', split_axis=2, conc...  5.88 us
    reduce_sum x1, other arithmetic, shards(): summed = jnp.sum(squared * phonon_occ[0, 0][:, None, None, :], axis=3)  3.71 us
    gather x4, local copies, waits for them, and re-layouts, shards(): local_terms = tile_terms(weight, jnp.take(rounded, kq_source[0, 0], axis=2))  2.44 us
  transfers between devices with their start and end apart: 2, of which 1 were waited for; matrix products, arithmetic and copies ran while one was open for 18% of the time, Pallas kernels for 0%

profile of v1, /device:TPU:0, one launch (start us, length us, event | category | flops | bytes accessed | tf_op | source)
XLA Modules:
  0.0 87.6 jit_solution(2420365117067099423)
XLA Ops:
  0.5 1.3 %reduce.10 = s32[32]{0:T(128)S(1)} reduce(s32[1,1,32]{2,1,0:T(1,128)} %param.14, s32[]{:T(128)} %broadcast.93), dimensions={0,1}, to_apply=%param.14.reduce_sub_computation.3 | reduce | bytes 260 | tf_op args[4]
  1.9 0.7 all_to_all.19
  2.5 7.4 %all-to-all-start.1 = ((s32[16,2,1]{1,2,0:T(1,128)}), s32[16,2,1]{1,2,0:T(1,128)S(1)}, u32[]{:S(2)}, u32[]{:S(2)}) async-start(s32[16,2,1]{1,2,0:T(1,128)} %bitcast.6), calls=%async_computation.1 | async-start | bytes 16384 | tf_op jit(solution)/shard_map/all_to_all | solution.py:30
  10.0 0.7 compare_select_fusion
  10.6 0.7 compare_and_fusion
  11.3 1.3 %convert_multiply_fusion = f32[1,1,32,32,384]{4,3,2,1,0:T(8,128)S(1)} fusion(bf16[1,1,32,32,384]{4,3,2,1,0:T(8,128)(2,1)} %param.10), kind=kLoop, calls=%fused_computation.5 | loop fusion | flops 786432 | bytes 2359296 | tf_op jit(solution)/shard_map/mul | solution.py:27
  12.6 5.9 %copy.42 = f32[1,1,32,32,384]{3,2,4,1,0:T(8,128)} copy(f32[1,1,32,32,384]{4,3,2,1,0:T(8,128)S(1)} %convert_multiply_fusion) | data formatting | bytes 3145728 | tf_op jit(solution)/shard_map/mul | solution.py:27
  18.8 3.7 %multiply_reduce_fusion = f32[32,32,32]{1,0,2:T(8,128)S(1)} fusion(f32[32,32,32,12]{1,0,3,2:T(8,128)} %bitcast.47, f32[32,12]{0,1:T(8,128)S(1)} %bitcast.52), kind=kLoop, calls=%fused_computation.4 | loop fusion | flops 753664 | bytes 1705472 | tf_op jit(solution)/shard_map/reduce_sum | solution.py:28
  23.1 0.6 gather_fusion
  23.7 0.9 %fusion = bf16[3,32,32]{1,0,2:T(4,128)(2,1)} fusion(bf16[32,32,32]{2,1,0:T(8,128)(2,1)S(1)} %copy.43, bf16[32,3,32]{2,1,0:T(4,128)(2,1)S(1)} %gather_fusion, pred[32]{0:T(512)(128)(4,1)S(1)} %compare_and_fusion), kind=kOutput, calls=%fused_computation.14 | convolution fusion | flops 202752 | bytes 77856 | tf_op jit(solution)/shard_map/tnm,dmt->dnt/dot_general | solution.py:12
  24.7 6.0 %all-to-all-start = ((bf16[3,32,32]{1,0,2:T(4,128)(2,1)}), bf16[3,32,32]{1,0,2:T(4,128)(2,1)S(1)}, u32[]{:S(2)}, u32[]{:S(2)}) async-start(bf16[3,32,32]{1,0,2:T(4,128)(2,1)} %fusion), calls=%async_computation | async-start | bytes 65536 | tf_op jit(solution)/shard_map/all_to_all | solution.py:38
  30.7 0.7 reduce.11
  31.5 5.9 %all-to-all-done = bf16[3,32,32]{1,0,2:T(4,128)(2,1)S(1)} async-done(((bf16[3,32,32]{1,0,2:T(4,128)(2,1)}), bf16[3,32,32]{1,0,2:T(4,128)(2,1)S(1)}, u32[]{:S(2)}, u32[]{:S(2)}) %all-to-all-start) | async-done | bytes 6176 | tf_op jit(solution)/shard_map/all_to_all | solution.py:38
  37.5 4.5 %all-gather = bf16[6,32,128]{2,1,0:T(8,128)(2,1)S(1)} all-gather(bf16[3,32,128]{2,1,0:T(8,128)(2,1)S(1)} %convolution_convert_fusion.7), channel_id=2, replica_groups=mesh['pb'=2,'ka'=16] {'pb'}, dimensions={0}, use_global_device_ids=true | all-gather | bytes 73728 | tf_op jit(solution)/shard_map/all_gather | solution.py:49
  42.2 0.6 gather_fusion.1
  43.1 9.2 %all_to_all.29 = bf16[3,32,32]{1,0,2:T(4,128)(2,1)S(1)} all-to-all(bf16[3,32,32]{1,0,2:T(4,128)(2,1)S(1)} %fusion.1), channel_id=1, replica_groups=mesh['pb'=2,'ka'=16] {'ka'}, dimensions={2} | all-to-all | bytes 12288 | tf_op jit(solution)/shard_map/all_to_all | solution.py:38
  52.5 4.5 %all-gather.1 = bf16[6,32,128]{2,1,0:T(8,128)(2,1)S(1)} all-gather(bf16[3,32,128]{2,1,0:T(8,128)(2,1)S(1)} %convolution_convert_fusion.6), channel_id=3, replica_groups=mesh['pb'=2,'ka'=16] {'pb'}, dimensions={0}, use_global_device_ids=true | all-gather | bytes 73728 | tf_op jit(solution)/shard_map/all_gather | solution.py:49
  57.2 0.6 gather_fusion.2
  58.1 9.2 %all_to_all.30 = bf16[3,32,32]{1,0,2:T(4,128)(2,1)S(1)} all-to-all(bf16[3,32,32]{1,0,2:T(4,128)(2,1)S(1)} %fusion.2), channel_id=1, replica_groups=mesh['pb'=2,'ka'=16] {'ka'}, dimensions={2} | all-to-all | bytes 12288 | tf_op jit(solution)/shard_map/all_to_all | solution.py:38
  67.5 4.5 %all-gather.2 = bf16[6,32,128]{2,1,0:T(8,128)(2,1)S(1)} all-gather(bf16[3,32,128]{2,1,0:T(8,128)(2,1)S(1)} %convolution_convert_fusion.5), channel_id=4, replica_groups=mesh['pb'=2,'ka'=16] {'pb'}, dimensions={0}, use_global_device_ids=true | all-gather | bytes 73728 | tf_op jit(solution)/shard_map/all_gather | solution.py:49
  72.1 0.6 gather_fusion.3
  73.1 9.2 %all_to_all.31 = bf16[3,32,32]{1,0,2:T(4,128)(2,1)S(1)} all-to-all(bf16[3,32,32]{1,0,2:T(4,128)(2,1)S(1)} %fusion.3), channel_id=1, replica_groups=mesh['pb'=2,'ka'=16] {'ka'}, dimensions={2} | all-to-all | bytes 12288 | tf_op jit(solution)/shard_map/all_to_all | solution.py:38
  82.5 4.5 %all-gather.3 = bf16[6,32,128]{2,1,0:T(8,128)(2,1)S(1)} all-gather(bf16[3,32,128]{2,1,0:T(8,128)(2,1)S(1)} %convolution_convert_fusion.4), channel_id=5, replica_groups=mesh['pb'=2,'ka'=16] {'pb'}, dimensions={0}, use_global_device_ids=true | all-gather | bytes 73728 | tf_op jit(solution)/shard_map/all_gather | solution.py:49
  87.0 0.6 add_multiply_fusion
  (39 shorter events, 3.6 us)
Async XLA Ops:
  0.0 18.6 %copy-start.3 = (f32[1,1,32,12]{2,1,3,0:T(1,128)S(1)}, f32[1,1,32,12]{2,1,3,0:T(1,128)}, u32[]{:S(2)}) copy-start(f32[1,1,32,12]{2,1,3,0:T(1,128)} %param.11) | copy-start | bytes 4612
  0.0 18.6 %copy-start.4 = (s32[1,1,16]{2,1,0:T(1,128)S(1)}, s32[1,1,16]{2,1,0:T(1,128)}, u32[]{:S(2)}) copy-start(s32[1,1,16]{2,1,0:T(1,128)} %param.13) | copy-start | bytes 196
  2.5 22.1 %all-to-all-start.1 = ((s32[16,2,1]{1,2,0:T(1,128)}), s32[16,2,1]{1,2,0:T(1,128)S(1)}, u32[]{:S(2)}, u32[]{:S(2)}) async-start(s32[16,2,1]{1,2,0:T(1,128)} %bitcast.6), calls=%async_computation.1 | async-start | bytes 16384 | tf_op jit(solution)/shard_map/all_to_all | solution.py:30
  12.6 9.9 %copy-start.2 = (s32[1,1,32,32]{3,2,1,0:T(8,128)S(1)}, s32[1,1,32,32]{3,2,1,0:T(8,128)}, u32[]{:S(2)}) copy-start(s32[1,1,32,32]{3,2,1,0:T(8,128)} %param.12) | copy-start | bytes 12292
  12.6 10.3 %copy-start = (f32[3,32,128]{2,1,0:T(8,128)S(1)}, f32[3,32,128]{2,1,0:T(8,128)}, u32[]{:S(2)}) copy-start(f32[3,32,128]{2,1,0:T(8,128)} %param.16) | copy-start | bytes 147460
  12.6 10.3 %copy-start.1 = (f32[32,128]{1,0:T(8,128)S(1)}, f32[32,128]{1,0:T(8,128)}, u32[]{:S(2)}) copy-start(f32[32,128]{1,0:T(8,128)} %param.17) | copy-start | bytes 49156
  24.7 12.6 %all-to-all-start = ((bf16[3,32,32]{1,0,2:T(4,128)(2,1)}), bf16[3,32,32]{1,0,2:T(4,128)(2,1)S(1)}, u32[]{:S(2)}, u32[]{:S(2)}) async-start(bf16[3,32,32]{1,0,2:T(4,128)(2,1)} %fusion), calls=%async_computation | async-start | bytes 65536 | tf_op jit(solution)/shard_map/all_to_all | solution.py:38
